TPU v7x, 32 devices: a whole 2x2x4 slice. The times are simulated.
32 devices in a mesh: row: 8 (over y, x, core), col: 4 (over z).
Axes of the slice: x: 2, y: 2, z: 4, core: 2. Of those that a mesh axis runs over, the one named last changes fastest.
Arguments:
- query: bfloat16 [8, 512, 4096], P(None, 'col'), may hold values from -7 to 7
- key: bfloat16 [4096, 512], P(('row', 'col')), may hold values from -7 to 7
- value: bfloat16 [4096, 512], P(('row', 'col')), may hold values from -4 to 4
- span_order: int32 [32], replicated, may hold values from 0 to 31, each once
Outputs:
- attention: bfloat16 [4096, 4096], P(('row', 'col'))
Inputs may be any that keep to these rules, and one draw needn't show every extreme that they name: span_order is a permutation of 0 to 31.
All inputs are finite; a program needn't handle non-finite values.
Results may differ from a plain program's by a relative error of at most 0.0085.
Values may be sent and summed in bfloat16 or wider, within the bound.
A program may use at most 192 MiB of HBM per device.

v0:
```python
import functools
import math

import jax
import jax.numpy as jnp
from jax import lax
from jax.experimental import pallas as pl
from jax.experimental.pallas import tpu as pltpu
from jax.sharding import PartitionSpec as P

HEAD_DIM = 128
KVHEADS = 4
SIDE = 2
masked_score = -1e30
MESH = pl.DeviceIdType.MESH
VMEM_LIMIT = 60 * 1024 * 1024
ONES = 16
SCALE = math.log2(math.e) / math.sqrt(HEAD_DIM)


def device(row, col):
    return {"row": row, "col": col}


def fused_kernel(rows, cols, heads, order_hbm, query_hbm, key_hbm, value_hbm, out_ref,
                 order_ref, query_ref, key_ref, value_ref, turned, held, queries, scores_even, scores_odd,
                 total, best, tops, lower, stage,
                 load_sem, plane_send, plane_recv, col_send, col_recv, side_send, side_recv,
                 own_sem, part_send, part_recv):
    share = rows // KVHEADS
    tokens = key_ref.shape[0]
    width = heads * tokens
    block = 2 * tokens
    blocks = rows * tokens // block
    units = rows * cols
    row, col = lax.axis_index("row"), lax.axis_index("col")
    head, lane = row // share, row % share
    ways = (1, -1)

    here = pl.ds(pl.multiple_of(head * HEAD_DIM, HEAD_DIM), HEAD_DIM)
    mine = pl.ds(pl.multiple_of(row * width, width), width)
    loads = [
        pltpu.make_async_copy(value_hbm, value_ref, load_sem.at[0]),
        pltpu.make_async_copy(key_hbm, key_ref, load_sem.at[1]),
        pltpu.make_async_copy(key_hbm.at[:, here], held.at[col, row, 0], load_sem.at[2]),
        pltpu.make_async_copy(order_hbm, order_ref, load_sem.at[3]),
        pltpu.make_async_copy(query_hbm.at[:, :, mine], query_ref, load_sem.at[4]),
    ]
    for load in loads:
        load.start()

    barrier = pltpu.get_barrier_semaphore()
    for step in range(1, rows):
        pl.semaphore_signal(
            barrier, inc=1, device_id=device(lax.rem(row + step, rows), col), device_id_type=MESH
        )
    for way in ways:
        @pl.when(jnp.logical_and(col + way >= 0, col + way < cols))
        def _(way=way):
            pl.semaphore_signal(barrier, inc=1, device_id=device(row, col + way), device_id_type=MESH)

    ends = jnp.where(col == 0, 1, 0) + jnp.where(col == cols - 1, 1, 0)

    def chip_at(step):
        along = lax.rem(head % SIDE + step % SIDE, SIDE)
        return lax.rem(head // SIDE + step // SIDE, SIDE) * SIDE + along

    loads[0].wait()
    for other in range(KVHEADS):
        turned[other] = value_ref[:, other * HEAD_DIM : (other + 1) * HEAD_DIM].T
    held[col, row, 1] = turned[head]
    loads[1].wait()
    loads[2].wait()
    pl.semaphore_wait(barrier, rows - 1 + len(ways) - ends)

    plane = []
    for step in range(1, KVHEADS):
        other = chip_at(step)
        columns = pl.ds(pl.multiple_of(other * HEAD_DIM, HEAD_DIM), HEAD_DIM)
        for kind, source in enumerate((key_ref.at[:, columns], turned.at[other])):
            copy = pltpu.make_async_remote_copy(
                src_ref=source,
                dst_ref=held.at[col, row, kind],
                send_sem=plane_send.at[step - 1, kind],
                recv_sem=plane_recv.at[step - 1, kind],
                device_id=device(other * share + lane, col),
                device_id_type=MESH,
            )
            copy.start()
            plane.append(copy)

    def plane_in(piece, kind):
        spot = held.at[col, chip_at(piece) * share + lane, kind]
        return pltpu.make_async_remote_copy(
            src_ref=spot,
            dst_ref=spot,
            send_sem=plane_send.at[piece - 1, kind],
            recv_sem=plane_recv.at[piece - 1, kind],
            device_id=device(chip_at(piece) * share + lane, col),
            device_id_type=MESH,
        )

    def held_here(step, way):
        source = col - way * step
        return jnp.logical_and(source >= 0, source < cols)

    def passes_on(step, way):
        target = col + way
        return jnp.logical_and(held_here(step, way), jnp.logical_and(target >= 0, target < cols))

    def col_copy(step, way, piece, arriving):
        source = col - way * (step + 1) if arriving else col - way * step
        spot = held.at[source, chip_at(piece) * share + lane]
        return pltpu.make_async_remote_copy(
            src_ref=spot,
            dst_ref=spot,
            send_sem=col_send.at[step, ways.index(way), piece],
            recv_sem=col_recv.at[step, ways.index(way), piece],
            device_id=device(row, col - way if arriving else col + way),
            device_id_type=MESH,
        )

    def side_copy(source, piece, other, arriving):
        there = lax.rem(lane - other + share, share) if arriving else lane
        spot = held.at[source, chip_at(piece) * share + there]
        return pltpu.make_async_remote_copy(
            src_ref=spot,
            dst_ref=spot,
            send_sem=side_send.at[source, piece, other - 1],
            recv_sem=side_recv.at[source, piece, other - 1],
            device_id=device(head * share + lax.rem(lane + other, share), col),
            device_id_type=MESH,
        )

    def relay(step, piece):
        for way in ways:
            if step:
                @pl.when(held_here(step, way))
                def _(way=way):
                    col_copy(step - 1, way, piece, True).wait_recv()

            if step < cols - 1:
                @pl.when(passes_on(step, way))
                def _(way=way):
                    col_copy(step, way, piece, False).start()

            if step or way == 1:
                @pl.when(held_here(step, way))
                def _(way=way):
                    for other in range(1, share):
                        side_copy(col - way * step, piece, other, False).start()

    for piece in range(KVHEADS):
        if piece:
            plane_in(piece, 0).wait_recv()
            plane_in(piece, 1).wait_recv()
        relay(0, piece)

    loads[4].wait()
    for index in range(rows):
        for member in range(heads):
            queries[index, :, member * tokens : (member + 1) * tokens] = query_ref[
                index, :, member * HEAD_DIM : (member + 1) * HEAD_DIM
            ].T
    across = lax.broadcasted_iota(jnp.int32, (tokens, tokens), 1)
    lower[...] = lax.broadcasted_iota(jnp.int32, (tokens, tokens), 0) - across
    loads[3].wait()

    left, right = col, cols - 1 - col
    both = jnp.minimum(left, right)

    def plane_of(phase):
        near = (phase + 1) // 2
        paired = jnp.where(phase % 2 == 1, col - near, col + near)
        far = phase - both
        single = jnp.where(left > right, col - far, col + far)
        return jnp.where(phase <= 2 * both, paired, single)

    def block_of(turn):
        half = share // 2
        slot, part = turn // half, half - 1 - turn % half
        outer = 1 - slot // 6
        along = outer * (1 - (slot % 2) * (slot // 3))
        down = outer * (1 - ((slot + 1) % 2) * ((slot + 1) // 3))
        shift = jnp.where(slot < 2, slot, jnp.where(slot < 6, slot // 4, 7 - slot))
        chip = lax.rem(head // SIDE + down, SIDE) * SIDE + lax.rem(head % SIDE + along, SIDE)
        return chip * share + lax.rem(lane + shift * half + part, share)

    def ready(phase):
        source = plane_of(phase) if phase else col
        for piece in range(KVHEADS):
            for other in range(1, share):
                side_copy(source, piece, other, True).wait_recv()

    def produce(phase, turn, part, buffer, newest):
        source = plane_of(phase) if phase else col
        index = block_of(turn)
        place = order_ref[index * cols + col]
        keys = held[source, 2 * part : 2 * part + 2, 0].reshape(block, HEAD_DIM)
        scores = jnp.dot(keys, queries[index], preferred_element_type=jnp.float32)
        for half in range(2):
            span = 2 * part + half
            lines = scores[half * tokens : (half + 1) * tokens]
            if phase == 0:
                limit = jnp.where(index == span, 0, tokens)
                shown = jnp.concatenate([lower[...]] * heads, axis=1) <= limit
                lines = jnp.where(shown, lines, masked_score)
            buffer[span * tokens : (span + 1) * tokens, :] = lines
            top = jnp.max(lines.reshape(tokens // 8, 8, width), axis=0)
            newest = jnp.maximum(newest, jnp.where(order_ref[span * cols + source] <= place, top, masked_score))
        return newest

    def consume(phase, turn, part, buffer, level, summed):
        source = plane_of(phase) if phase else col
        place = order_ref[block_of(turn) * cols + col]
        raised, columns = [], []
        for half in range(2):
            span = 2 * part + half
            ceiling = jnp.where(order_ref[span * cols + source] <= place, level, -masked_score)
            lines = buffer[span * tokens : (span + 1) * tokens, :]
            raised.append(jnp.exp2(lines * SCALE - ceiling).astype(jnp.bfloat16))
            columns.append(held[source, span, 1])
        ones = jnp.ones((ONES, block), jnp.bfloat16)
        weighed = jnp.concatenate([jnp.concatenate(columns, axis=1), ones], axis=0)
        update = jnp.dot(weighed, jnp.concatenate(raised, axis=0), preferred_element_type=jnp.float32)
        return update if summed is None else summed + update

    def first(phase, turn, buffer):
        newest = jnp.full((8, width), masked_score, jnp.float32)
        for part in range(blocks):
            newest = produce(phase, turn, part, buffer, newest)
        tops[...] = newest

    def unit(phase, turn, now, later, following):
        index = block_of(turn)
        highest = jnp.max(tops[...], axis=0, keepdims=True)
        if phase:
            before = best[index, 0:1, :]
            highest = jnp.maximum(before, highest)
            shrink = jnp.exp2((before - highest) * SCALE)
        level = highest * SCALE
        best[index] = jnp.broadcast_to(highest, (8, width))
        newest = jnp.full((8, width), masked_score, jnp.float32)
        summed = None
        for part in range(blocks):
            if following is not None:
                newest = produce(*following, part, later, newest)
            summed = consume(phase, turn, part, now, level, summed)
        if following is not None:
            tops[...] = newest
        if phase:
            summed = total[index] * shrink + summed
        if phase < cols - 1:
            total[index] = summed
        else:
            share_of = summed[:HEAD_DIM] / summed[HEAD_DIM : HEAD_DIM + 1]
            for member in range(heads):
                stage[turn, :, member * HEAD_DIM : (member + 1) * HEAD_DIM] = (
                    share_of[:, member * tokens : (member + 1) * tokens].T.astype(stage.dtype)
                )

    def part_copy(turn):
        return pltpu.make_async_remote_copy(
            src_ref=stage.at[turn],
            dst_ref=out_ref.at[:, mine],
            send_sem=part_send.at[turn],
            recv_sem=part_recv.at[turn],
            device_id=device(block_of(turn), col),
            device_id_type=MESH,
        )

    pairs = rows // 2
    ready(0)
    first(0, 0, scores_even)
    for phase in range(cols):
        final = phase == cols - 1

        def body(pair, carry, phase=phase, final=final):
            turn = 2 * pair
            if not final:
                for piece in range(KVHEADS):
                    @pl.when(pair == (piece + 1) * pairs // (KVHEADS + 1))
                    def _(piece=piece):
                        relay(phase + 1, piece)
            unit(phase, turn, scores_even, scores_odd, (phase, turn + 1))
            if final:
                part_copy(turn).start()
            unit(phase, turn + 1, scores_odd, scores_even, (phase, turn + 2))
            if final:
                part_copy(turn + 1).start()
            return carry

        lax.fori_loop(0, pairs - 1, body, 0)
        turn = rows - 2
        if not final:
            for piece in range(KVHEADS):
                if (piece + 1) * pairs // (KVHEADS + 1) >= pairs - 1:
                    relay(phase + 1, piece)
        unit(phase, turn, scores_even, scores_odd, (phase, turn + 1))
        if final:
            part_copy(turn).start()
            unit(phase, turn + 1, scores_odd, scores_even, None)
        else:
            ready(phase + 1)
            unit(phase, turn + 1, scores_odd, scores_even, (phase + 1, 0))

    own = pltpu.make_async_copy(stage.at[rows - 1], out_ref.at[:, mine], own_sem)
    own.start()
    for copy in plane:
        copy.wait_send()
    for step in range(cols):
        for way in ways:
            if step < cols - 1:
                @pl.when(passes_on(step, way))
                def _(way=way):
                    for piece in range(KVHEADS):
                        col_copy(step, way, piece, False).wait_send()

            if step or way == 1:
                @pl.when(held_here(step, way))
                def _(way=way):
                    for piece in range(KVHEADS):
                        for other in range(1, share):
                            side_copy(col - way * step, piece, other, False).wait_send()
    own.wait()
    for turn in range(rows - 1):
        part_copy(turn).wait()


def fused(query, key, value, span_order, rows, cols):
    tokens = key.shape[0]
    share = rows // KVHEADS
    width = query.shape[2] // rows
    heads = width // HEAD_DIM
    lines = heads * tokens
    kind = query.dtype
    real = jnp.float32
    dma = pltpu.SemaphoreType.DMA
    return pl.pallas_call(
        functools.partial(fused_kernel, rows, cols, heads),
        out_shape=jax.ShapeDtypeStruct((tokens, rows * width), kind),
        in_specs=[pl.BlockSpec(memory_space=pl.ANY)] * 4,
        out_specs=pl.BlockSpec(memory_space=pl.ANY),
        scratch_shapes=[
            pltpu.SMEM(span_order.shape, jnp.int32),
            pltpu.VMEM((rows, tokens, width), kind),
            pltpu.VMEM(key.shape, kind),
            pltpu.VMEM(value.shape, kind),
            pltpu.VMEM((KVHEADS, HEAD_DIM, tokens), kind),
            pltpu.VMEM((cols, rows, 2, tokens, HEAD_DIM), kind),
            pltpu.VMEM((rows, HEAD_DIM, lines), kind),
            pltpu.VMEM((rows * tokens, lines), real),
            pltpu.VMEM((rows * tokens, lines), real),
            pltpu.VMEM((rows, HEAD_DIM + ONES, lines), real),
            pltpu.VMEM((rows, 8, lines), real),
            pltpu.VMEM((8, lines), real),
            pltpu.VMEM((tokens, tokens), jnp.int32),
            pltpu.VMEM((rows, tokens, width), kind),
            dma((5,)),
            dma((KVHEADS - 1, 2)),
            dma((KVHEADS - 1, 2)),
            dma((cols - 1, 2, KVHEADS)),
            dma((cols - 1, 2, KVHEADS)),
            dma((cols, KVHEADS, share - 1)),
            dma((cols, KVHEADS, share - 1)),
            dma(()),
            dma((rows - 1,)),
            dma((rows - 1,)),
        ],
        compiler_params=pltpu.CompilerParams(
            collective_id=0, has_side_effects=True, vmem_limit_bytes=VMEM_LIMIT
        ),
        name="fused",
    )(span_order, query, key, value)


def shards(query, key, value, span_order):
    return fused(query, key, value, span_order, lax.axis_size("row"), lax.axis_size("col"))


def solution(mesh):
    placed = (P(None, "col", None), P(("row", "col"), None), P(("row", "col"), None), P())
    return jax.shard_map(
        shards, mesh=mesh, in_specs=placed, out_specs=P(("row", "col"), None), check_vma=False
    )
```

profile of v0, /device:TPU:1, one launch (start us, length us, event | category | flops | bytes accessed | tf_op | source)
XLA Modules:
  0.0 45.5 jit_solution(6959875255207127802)
XLA Ops:
  0.0 43.2 %fused.1 = bf16[128,4096]{1,0:T(8,128)(2,1)} custom-call(s32[32]{0:T(128)} %order_hbm.1, bf16[8,128,4096]{2,1,0:T(8,128)(2,1)} %query_hbm.1, bf16[128,512]{1,0:T(8,128)(2,1)} %key_hbm.1, bf16[128,512]{1,0:T(8,128)(2,1)} %value_hbm.1), custom_call_target="tpu_custom_call" | custom-call | tf_op jit(solution)/shard_map/fused/pallas_call | solution.py:339
  43.3 2.3 %copy.6 = bf16[128,4096]{1,0:T(8,128)(2,1)} copy(bf16[128,4096]{1,0:T(8,128)(2,1)} %fused.1) | data formatting | bytes 2097152
where the time goes:
time: 46.1 us; the launch traced here: 45.5 us
  Pallas kernels  43.2 us (94%)
  local copies, waits for them, and re-layouts  2.29 us (5%)
    pallas_call x1, Pallas kernels, fused(): pl.pallas_call(functools.partial(fused_kernel, rows, cols, heads), out_sh...  43.2 us
    unnamed x1, local copies, waits for them, and re-layouts  2.29 us

commit v1 on v0

--- a/solution.py
+++ b/solution.py
@@ -13,9 +13,11 @@
 SIDE = 2
 masked_score = -1e30
 MESH = pl.DeviceIdType.MESH
-VMEM_LIMIT = 60 * 1024 * 1024
+VMEM_LIMIT = 40 * 1024 * 1024
 ONES = 16
 SCALE = math.log2(math.e) / math.sqrt(HEAD_DIM)
+TILE = 256
+POS = (0, 2, 2, 4)
 
 
 def device(row, col):
@@ -31,8 +33,7 @@
     tokens = key_ref.shape[0]
     width = heads * tokens
     block = 2 * tokens
-    blocks = rows * tokens // block
-    units = rows * cols
+    tile = min(width, TILE)
     row, col = lax.axis_index("row"), lax.axis_index("col")
     head, lane = row // share, row % share
     ways = (1, -1)
@@ -150,18 +151,22 @@
                     for other in range(1, share):
                         side_copy(col - way * step, piece, other, False).start()
 
-    for piece in range(KVHEADS):
+    def relay_own(piece):
         if piece:
             plane_in(piece, 0).wait_recv()
             plane_in(piece, 1).wait_recv()
         relay(0, piece)
 
+    relay_own(0)
     loads[4].wait()
     for index in range(rows):
         for member in range(heads):
-            queries[index, :, member * tokens : (member + 1) * tokens] = query_ref[
-                index, :, member * HEAD_DIM : (member + 1) * HEAD_DIM
-            ].T
+            part = query_ref[index, :, member * HEAD_DIM : (member + 1) * HEAD_DIM].astype(jnp.float32) * SCALE
+            high = part.astype(queries.dtype)
+            low = (part - high.astype(jnp.float32)).astype(queries.dtype)
+            lines = slice(member * tokens, (member + 1) * tokens)
+            queries[index, :HEAD_DIM, lines] = high.T
+            queries[index, HEAD_DIM:, lines] = low.T
     across = lax.broadcasted_iota(jnp.int32, (tokens, tokens), 1)
     lower[...] = lax.broadcasted_iota(jnp.int32, (tokens, tokens), 0) - across
     loads[3].wait()
@@ -179,85 +184,108 @@
     def block_of(turn):
         half = share // 2
         slot, part = turn // half, half - 1 - turn % half
+        straight = 1 - jnp.minimum(slot // 4, 1)
         outer = 1 - slot // 6
-        along = outer * (1 - (slot % 2) * (slot // 3))
-        down = outer * (1 - ((slot + 1) % 2) * ((slot + 1) // 3))
-        shift = jnp.where(slot < 2, slot, jnp.where(slot < 6, slot // 4, 7 - slot))
+        along = outer * (1 - straight * (slot % 2))
+        down = outer * (1 - straight * (1 - slot % 2))
+        shift = jnp.where(slot < 4, slot // 2, jnp.where(slot < 6, slot % 2, 7 - slot))
         chip = lax.rem(head // SIDE + down, SIDE) * SIDE + lax.rem(head % SIDE + along, SIDE)
         return chip * share + lax.rem(lane + shift * half + part, share)
 
-    def ready(phase):
-        source = plane_of(phase) if phase else col
-        for piece in range(KVHEADS):
+    def parts_of(step):
+        source = plane_of(step) if step else col
+        return [
+            (step, source, [chip_at(piece) * share + 2 * half + one for one in range(2)])
+            for piece in range(KVHEADS)
+            for half in range(share // 2)
+        ]
+
+    def ready(step, start, stop):
+        source = plane_of(step) if step else col
+        for piece in range(start, stop):
             for other in range(1, share):
                 side_copy(source, piece, other, True).wait_recv()
 
-    def produce(phase, turn, part, buffer, newest):
-        source = plane_of(phase) if phase else col
+    def produce(part, number, turn, cut, buffer, newest):
+        near, source, spans = part
         index = block_of(turn)
         place = order_ref[index * cols + col]
-        keys = held[source, 2 * part : 2 * part + 2, 0].reshape(block, HEAD_DIM)
-        scores = jnp.dot(keys, queries[index], preferred_element_type=jnp.float32)
-        for half in range(2):
-            span = 2 * part + half
+        keys = held[source, pl.ds(spans[0], 2), 0].reshape(block, HEAD_DIM)
+        scores = jnp.dot(
+            jnp.concatenate([keys, keys], axis=1), queries[index, :, cut], preferred_element_type=jnp.float32
+        )
+        for half, span in enumerate(spans):
             lines = scores[half * tokens : (half + 1) * tokens]
-            if phase == 0:
+            if near == 0:
                 limit = jnp.where(index == span, 0, tokens)
-                shown = jnp.concatenate([lower[...]] * heads, axis=1) <= limit
+                shown = jnp.concatenate([lower[...]] * (tile // tokens), axis=1) <= limit
                 lines = jnp.where(shown, lines, masked_score)
-            buffer[span * tokens : (span + 1) * tokens, :] = lines
-            top = jnp.max(lines.reshape(tokens // 8, 8, width), axis=0)
+            spot = (2 * number + half) * tokens
+            buffer[spot : spot + tokens, cut] = lines
+            top = jnp.max(lines.reshape(tokens // 8, 8, tile), axis=0)
             newest = jnp.maximum(newest, jnp.where(order_ref[span * cols + source] <= place, top, masked_score))
         return newest
 
-    def consume(phase, turn, part, buffer, level, summed):
-        source = plane_of(phase) if phase else col
+    def consume(part, number, turn, cut, buffer, level, summed):
+        near, source, spans = part
         place = order_ref[block_of(turn) * cols + col]
         raised, columns = [], []
-        for half in range(2):
-            span = 2 * part + half
+        for half, span in enumerate(spans):
             ceiling = jnp.where(order_ref[span * cols + source] <= place, level, -masked_score)
-            lines = buffer[span * tokens : (span + 1) * tokens, :]
-            raised.append(jnp.exp2(lines * SCALE - ceiling).astype(jnp.bfloat16))
+            spot = (2 * number + half) * tokens
+            raised.append(jnp.exp2(buffer[spot : spot + tokens, cut] - ceiling).astype(held.dtype))
             columns.append(held[source, span, 1])
-        ones = jnp.ones((ONES, block), jnp.bfloat16)
+        ones = jnp.ones((ONES, block), held.dtype)
         weighed = jnp.concatenate([jnp.concatenate(columns, axis=1), ones], axis=0)
         update = jnp.dot(weighed, jnp.concatenate(raised, axis=0), preferred_element_type=jnp.float32)
         return update if summed is None else summed + update
 
-    def first(phase, turn, buffer):
-        newest = jnp.full((8, width), masked_score, jnp.float32)
-        for part in range(blocks):
-            newest = produce(phase, turn, part, buffer, newest)
-        tops[...] = newest
-
-    def unit(phase, turn, now, later, following):
+    cuts = [slice(start, start + tile) for start in range(0, width, tile)]
+
+    def first(buffer):
+        for cut in cuts:
+            newest = jnp.full((8, tile), masked_score, jnp.float32)
+            for number, part in enumerate(parts_of(0)):
+                newest = produce(part, number, 0, cut, buffer, newest)
+            tops[:, cut] = newest
+
+    def unit(step, turn, now, later, following, late=0):
         index = block_of(turn)
+        parts = parts_of(step)
+        coming = [] if following is None else parts_of(following[0])
         highest = jnp.max(tops[...], axis=0, keepdims=True)
-        if phase:
+        if step:
             before = best[index, 0:1, :]
             highest = jnp.maximum(before, highest)
-            shrink = jnp.exp2((before - highest) * SCALE)
-        level = highest * SCALE
+            shrink = jnp.exp2(before - highest)
         best[index] = jnp.broadcast_to(highest, (8, width))
-        newest = jnp.full((8, width), masked_score, jnp.float32)
-        summed = None
-        for part in range(blocks):
+        for cut in cuts:
+            newest = jnp.full((8, tile), masked_score, jnp.float32)
+            summed = None
+            for number in range(len(parts)):
+                if number < len(coming) - late:
+                    newest = produce(coming[number], number, following[1], cut, later, newest)
+                summed = consume(parts[number], number, turn, cut, now, highest[:, cut], summed)
             if following is not None:
-                newest = produce(*following, part, later, newest)
-            summed = consume(phase, turn, part, now, level, summed)
-        if following is not None:
-            tops[...] = newest
-        if phase:
-            summed = total[index] * shrink + summed
-        if phase < cols - 1:
-            total[index] = summed
-        else:
-            share_of = summed[:HEAD_DIM] / summed[HEAD_DIM : HEAD_DIM + 1]
-            for member in range(heads):
-                stage[turn, :, member * HEAD_DIM : (member + 1) * HEAD_DIM] = (
-                    share_of[:, member * tokens : (member + 1) * tokens].T.astype(stage.dtype)
-                )
+                tops[:, cut] = newest
+            if step:
+                summed = total[index, :, cut] * shrink[:, cut] + summed
+            if step < cols - 1:
+                total[index, :, cut] = summed
+            else:
+                share_of = summed[:HEAD_DIM] / summed[HEAD_DIM : HEAD_DIM + 1]
+                for member in range(tile // tokens):
+                    spot = cut.start // tokens * HEAD_DIM + member * HEAD_DIM
+                    stage[turn, :, spot : spot + HEAD_DIM] = (
+                        share_of[:, member * tokens : (member + 1) * tokens].T.astype(stage.dtype)
+                    )
+
+    def rest(step, late, buffer):
+        for cut in cuts:
+            newest = tops[:, cut]
+            for number, part in list(enumerate(parts_of(step)))[-late:]:
+                newest = produce(part, number, 0, cut, buffer, newest)
+            tops[:, cut] = newest
 
     def part_copy(turn):
         return pltpu.make_async_remote_copy(
@@ -270,39 +298,54 @@
         )
 
     pairs = rows // 2
-    ready(0)
-    first(0, 0, scores_even)
-    for phase in range(cols):
-        final = phase == cols - 1
-
-        def body(pair, carry, phase=phase, final=final):
+    last = rows - 1
+    hooks = [[(POS[piece] * last // 7, step, piece) for piece in range(KVHEADS)] for step in range(1, cols)]
+    hooks += [[]]
+
+    def passing(step, piece):
+        if step:
+            relay(step, piece)
+        else:
+            relay_own(piece)
+
+    for piece in range(1,KVHEADS): relay_own(piece)
+    ready(0, 0, KVHEADS)
+    first(scores_even)
+    for step in range(cols):
+        final = step == cols - 1
+
+        def pass_at(turn, choices, step=step):
+            for when, which, piece in hooks[step]:
+                if when in choices:
+                    @pl.when(turn == when)
+                    def _(which=which, piece=piece):
+                        passing(which, piece)
+
+        def body(pair, carry, step=step, final=final, pass_at=pass_at):
             turn = 2 * pair
-            if not final:
-                for piece in range(KVHEADS):
-                    @pl.when(pair == (piece + 1) * pairs // (KVHEADS + 1))
-                    def _(piece=piece):
-                        relay(phase + 1, piece)
-            unit(phase, turn, scores_even, scores_odd, (phase, turn + 1))
+            pass_at(turn, range(0, last, 2))
+            unit(step, turn, scores_even, scores_odd, (step, turn + 1))
             if final:
                 part_copy(turn).start()
-            unit(phase, turn + 1, scores_odd, scores_even, (phase, turn + 2))
+            pass_at(turn + 1, range(1, last, 2))
+            unit(step, turn + 1, scores_odd, scores_even, (step, turn + 2))
             if final:
                 part_copy(turn + 1).start()
             return carry
 
         lax.fori_loop(0, pairs - 1, body, 0)
-        turn = rows - 2
-        if not final:
-            for piece in range(KVHEADS):
-                if (piece + 1) * pairs // (KVHEADS + 1) >= pairs - 1:
-                    relay(phase + 1, piece)
-        unit(phase, turn, scores_even, scores_odd, (phase, turn + 1))
+        turn = last - 1
+        pass_at(turn, (turn,))
+        unit(step, turn, scores_even, scores_odd, (step, last))
         if final:
             part_copy(turn).start()
-            unit(phase, turn + 1, scores_odd, scores_even, None)
+            unit(step, last, scores_odd, scores_even, None)
         else:
-            ready(phase + 1)
-            unit(phase, turn + 1, scores_odd, scores_even, (phase + 1, 0))
+            pass_at(last, (last,))
+            ready(step + 1, 0, KVHEADS - 1)
+            unit(step, last, scores_odd, scores_even, (step + 1, 0), share // 2)
+            ready(step + 1, KVHEADS - 1, KVHEADS)
+            rest(step + 1, share // 2, scores_even)
 
     own = pltpu.make_async_copy(stage.at[rows - 1], out_ref.at[:, mine], own_sem)
     own.start()
@@ -348,7 +391,7 @@
             pltpu.VMEM(value.shape, kind),
             pltpu.VMEM((KVHEADS, HEAD_DIM, tokens), kind),
             pltpu.VMEM((cols, rows, 2, tokens, HEAD_DIM), kind),
-            pltpu.VMEM((rows, HEAD_DIM, lines), kind),
+            pltpu.VMEM((rows, 2 * HEAD_DIM, lines), kind),
             pltpu.VMEM((rows * tokens, lines), real),
             pltpu.VMEM((rows * tokens, lines), real),
             pltpu.VMEM((rows, HEAD_DIM + ONES, lines), real),
@@ -371,11 +414,29 @@
             collective_id=0, has_side_effects=True, vmem_limit_bytes=VMEM_LIMIT
         ),
         name="fused",
-    )(span_order, query, key, value)
+    )(*(pltpu.with_memory_space_constraint(array, pltpu.HBM) for array in (span_order, query, key, value)))
+
+
+def finish_kernel(whole_ref, out_ref, sem):
+    copy = pltpu.make_async_copy(whole_ref, out_ref, sem)
+    copy.start()
+    copy.wait()
+
+
+def finish(whole):
+    return pl.pallas_call(
+        finish_kernel,
+        out_shape=jax.ShapeDtypeStruct(whole.shape, whole.dtype),
+        in_specs=[pl.BlockSpec(memory_space=pltpu.VMEM)],
+        out_specs=pl.BlockSpec(memory_space=pl.ANY),
+        scratch_shapes=[pltpu.SemaphoreType.DMA(())],
+        compiler_params=pltpu.CompilerParams(vmem_limit_bytes=4 * 1024 * 1024),
+        name="finish",
+    )(whole)
 
 
 def shards(query, key, value, span_order):
-    return fused(query, key, value, span_order, lax.axis_size("row"), lax.axis_size("col"))
+    return finish(fused(query, key, value, span_order, lax.axis_size("row"), lax.axis_size("col")))
 
 
 def solution(mesh):

time: 46.1 us -> 42.8 us (0.928)
  local copies, waits for them, and re-layouts: 2.29 us -> 0 us
  Pallas kernels: 43.2 us -> 42.7 us
    unnamed x1 -> x0, local copies, waits for them, and re-layouts: 2.29 us -> none
    pallas_call x1, Pallas kernels: 43.2 us -> 41.7 us  [fused(): pl.pallas_call(functools.partial(fused_kernel, rows, cols, heads), out_sh...]
    pallas_call x0 -> x1, Pallas kernels: none -> 0.98 us  [finish(): pl.pallas_call(finish_kernel, out_shape=jax.ShapeDtypeStruct(whole.shape,...]
where the time goes in v1:
time: 42.8 us; the launch traced here: 42.7 us
  Pallas kernels  42.7 us (100%)
    pallas_call x1, Pallas kernels, fused(): pl.pallas_call(functools.partial(fused_kernel, rows, cols, heads), out_sh...  41.7 us
    pallas_call x1, Pallas kernels, finish(): pl.pallas_call(finish_kernel, out_shape=jax.ShapeDtypeStruct(whole.shape,...  0.98 us

profile of v1, /device:TPU:1, one launch (start us, length us, event | category | flops | bytes accessed | tf_op | source)
XLA Modules:
  0.0 42.7 jit_solution(8379912069871553708)
XLA Ops:
  0.0 41.7 %fused.1.whole_ref = bf16[128,4096]{1,0:T(8,128)(2,1)S(1)} custom-call(s32[32]{0:T(128)} %order_hbm.1, bf16[8,128,4096]{2,1,0:T(8,128)(2,1)} %query_hbm.1, bf16[128,512]{1,0:T(8,128)(2,1)} %key_hbm.1, bf16[128,512]{1,0:T(8,128)(2,1)} %value_hbm.1), custom_call_target="tpu_custom_call" | custom-call | tf_op jit(solution)/shard_map/fused/pallas_call | solution.py:382
  41.7 1.0 %finish.1 = bf16[128,4096]{1,0:T(8,128)(2,1)} custom-call(bf16[128,4096]{1,0:T(8,128)(2,1)S(1)} %fused.1.whole_ref), custom_call_target="tpu_custom_call" | custom-call | tf_op jit(solution)/shard_map/finish/pallas_call | solution.py:427
